TPU v7x, 512 devices: a whole 4x4x16 slice. The times are simulated.
512 devices in a mesh: nodes: 128 (over z_hi, y, x, core), heads: 4 (over z_lo).
Axes of the slice: x: 4, y: 4, z: 16 (z_hi: 4, z_lo: 4; z = z_hi * 4 + z_lo), core: 2. Of those that a mesh axis runs over, the one named last changes fastest.
Arguments:
- grid_state: bfloat16 [131072, 1024], P('nodes', 'heads'), may hold values from -6 to 6
- mesh_state: bfloat16 [32768, 1024], P('nodes', 'heads'), may hold values from -6 to 6
- encoder_query: bfloat16 [1024, 512], P('nodes', 'heads'), may hold values from -0.1875 to 0.1875
- encoder_key: bfloat16 [1024, 512], P('nodes', 'heads'), may hold values from -0.1875 to 0.1875
- encoder_value: bfloat16 [1024, 512], P('nodes', 'heads'), may hold values from -0.1875 to 0.1875
- encoder_output: bfloat16 [512, 1024], P('heads', 'nodes'), may hold values from -0.25 to 0.25
- window_query: bfloat16 [1024, 512], P('nodes', 'heads'), may hold values from -0.1875 to 0.1875
- window_key: bfloat16 [1024, 512], P('nodes', 'heads'), may hold values from -0.1875 to 0.1875
- window_value: bfloat16 [1024, 512], P('nodes', 'heads'), may hold values from -0.1875 to 0.1875
- window_output: bfloat16 [512, 1024], P('heads', 'nodes'), may hold values from -0.25 to 0.25
- expand_weight: bfloat16 [1024, 2048], P('nodes', 'heads'), may hold values from -0.1875 to 0.1875
- shrink_weight: bfloat16 [2048, 1024], P('heads', 'nodes'), may hold values from -0.125 to 0.125
- decoder_query: bfloat16 [1024, 512], P('nodes', 'heads'), may hold values from -0.1875 to 0.1875
- decoder_key: bfloat16 [1024, 512], P('nodes', 'heads'), may hold values from -0.1875 to 0.1875
- decoder_value: bfloat16 [1024, 512], P('nodes', 'heads'), may hold values from -0.1875 to 0.1875
- decoder_output: bfloat16 [512, 1024], P('heads', 'nodes'), may hold values from -0.25 to 0.25
- encoder_blocks: int32 [256, 8], P('nodes'), may hold values from 0 to 1023, as said below
- encoder_count: int32 [256], P('nodes'), may hold values from 2 to 8, as said below
- window_offsets: int32 [256, 4], P('nodes'), may hold values from -2 to 2, as said below
- decoder_blocks: int32 [1024, 3], P('nodes'), may hold values from 0 to 255, as said below
- decoder_count: int32 [1024], P('nodes'), may hold values from 1 to 3, as said below
Outputs:
- grid_out: bfloat16 [131072, 1024], P('nodes', 'heads')
- mesh_out: bfloat16 [32768, 1024], P('nodes', 'heads')
Inputs may be any that keep to these rules, and one draw needn't show every extreme that they name: `encoder_blocks`: row m names 8 different grid blocks; each lies among the grid blocks of the index of nodes that holds mesh block m, or in the nearer half of the grid blocks of the index on either side. The first encoder_count[m] slots of row m are live; every mesh block held by the first or last eighth of the indices of nodes has all 8 slots live. `window_offsets`: each row holds 4 different offsets, the first of them 0. `decoder_blocks`: row g names 3 different mesh blocks; each lies among the mesh blocks of the index of nodes that holds grid block g, or is the one block next to them on either side. The first decoder_count[g] slots of row g are live; every grid block of the first index of nodes has all 3 slots live.
All inputs are finite; a program needn't handle non-finite values.
Results may differ from a plain program's by a relative error of at most 0.012.
Values may be sent and summed in bfloat16 or wider, within the bound.
No kernel may reach another device: no remote copies, remote signals or barrier semaphores. Data moves between devices by JAX's collectives and lax.ppermute only.
A program may use at most 64 MiB of HBM per device.

v0:
```python
import math
import jax
import jax.numpy as jnp
from jax import lax
from jax.sharding import PartitionSpec as P

HEAD_DIM = 64
TILE = 128
EPSILON = 1e-05


def turned_gather(arrays, axis, dims):
    turned = [jnp.moveaxis(a, dim, 0) for a, dim in zip(arrays, dims)]
    widths = [t[0].size for t in turned]
    both = jnp.concatenate([t.reshape(-1, w) for t, w in zip(turned, widths)], axis=1)
    whole = lax.all_gather(both, axis, axis=0, tiled=True)
    parts = jnp.split(whole, [sum(widths[:k]) for k in range(1, len(widths))], axis=1)
    return tuple(
        (
            jnp.moveaxis(b.reshape(-1, *t.shape[1:]), 0, dim)
            for b, t, dim in zip(parts, turned, dims)
        )
    )


def in_order(parts, dim):
    lengths = list(parts.shape[1:])
    lengths[dim] *= parts.shape[0]
    return jnp.moveaxis(parts, 0, dim).reshape(lengths)


def from_everyone(x, axis):
    length = lax.axis_size(axis)
    return lax.all_to_all(jnp.broadcast_to(x[None], (length, *x.shape)), axis, 0, 0, tiled=True)


def collect(x, axis, dim):
    return in_order(from_everyone(x, axis), dim)


def with_halo(x, sides, width):
    for axis, dim in sides:
        size, length = (lax.axis_size(axis), x.shape[dim])
        up = [(i, (i + 1) % size) for i in range(size - 1)]
        down = [(j, i) for i, j in up]
        last = lax.slice_in_dim(x, length - width, length, axis=dim)
        first = lax.slice_in_dim(x, 0, width, axis=dim)
        before = lax.ppermute(last, axis, up)
        after = lax.ppermute(first, axis, down)
        x = jnp.concatenate([before, x, after], axis=dim)
    return x


def in_blocks(x, dim, length):
    before, after = (x.shape[:dim], x.shape[dim + 1 :])
    return jnp.moveaxis(x.reshape(*before, length, -1, *after), dim, 0)


def sum_at_owner(x, axis, dim):
    parts = in_blocks(x, dim, lax.axis_size(axis))
    arrived = lax.all_to_all(parts, axis, split_axis=0, concat_axis=0, tiled=True)
    return arrived.astype(jnp.float32).sum(axis=0)


def normalize(values):
    values = values.astype(jnp.float32)
    average = jnp.mean(values, axis=-1, keepdims=True)
    centred = values - average
    spread = jnp.mean(centred * centred, axis=-1, keepdims=True)
    return (centred * lax.rsqrt(spread + EPSILON)).astype(jnp.bfloat16)


def local_terms(source, weight_list):
    return tuple(
        (jnp.dot(source, member, preferred_element_type=jnp.float32) for member in weight_list)
    )


def fold_parts(pieces, row_count):
    group_count = pieces.shape[0] // row_count
    return jnp.sum(pieces.reshape(group_count, row_count, pieces.shape[1]), axis=0)


def attend(queries, key_rows, value_rows, key_mask):
    batch_size, row_count, column_count = queries.shape
    head_count = column_count // HEAD_DIM
    split_query = queries.reshape(batch_size, row_count, head_count, HEAD_DIM)
    split_key = key_rows.reshape(batch_size, key_rows.shape[1], head_count, HEAD_DIM)
    split_value = value_rows.reshape(batch_size, value_rows.shape[1], head_count, HEAD_DIM)
    scores = jnp.einsum(
        "bqhd,bkhd->bhqk", split_query, split_key, preferred_element_type=jnp.float32
    )
    scores = jnp.where(key_mask[:, None, None, :], scores, -1e30)
    highest = jnp.max(scores, axis=-1, keepdims=True)
    weights = jnp.exp(scores - highest)
    weights = (weights / jnp.sum(weights, axis=-1, keepdims=True)).astype(jnp.bfloat16)
    mixture = jnp.einsum(
        "bhqk,bkhd->bqhd", weights, split_value, preferred_element_type=jnp.float32
    )
    return mixture.reshape(batch_size, row_count, column_count).astype(jnp.bfloat16)


def attend_blocks(queries, key_rows, value_rows, key_mask):
    tile_count = queries.shape[0]
    group_size = math.gcd(tile_count, 4)

    def one_group(arguments):
        return attend(arguments[0], arguments[1], arguments[2], arguments[3])

    grouped = tuple(
        (
            member.reshape((tile_count // group_size, group_size) + member.shape[1:])
            for member in (queries, key_rows, value_rows, key_mask)
        )
    )
    return lax.map(one_group, grouped).reshape(queries.shape)


def pick_tiles(stacked, tile_count, chosen):
    column_count = stacked.shape[-1]
    tile_view = stacked.reshape(2, tile_count, TILE, column_count)
    picked = jnp.take(tile_view, chosen, axis=1)
    shaped = picked.reshape(2, chosen.shape[0], chosen.shape[1] * TILE, column_count)
    return (shaped[0], shaped[1])


def slot_mask(live_count, slot_total):
    live = jnp.arange(slot_total, dtype=jnp.int32)[None, :] < live_count[:, None]
    return jnp.repeat(live, TILE, axis=1)


def local(
    grid_state,
    mesh_state,
    encoder_query,
    encoder_key,
    encoder_value,
    encoder_output,
    window_query,
    window_key,
    window_value,
    window_output,
    expand_weight,
    shrink_weight,
    decoder_query,
    decoder_key,
    decoder_value,
    decoder_output,
    encoder_blocks,
    encoder_count,
    window_offsets,
    decoder_blocks,
    decoder_count,
):
    scaling = HEAD_DIM ** (-0.5)
    position = lax.axis_index("nodes")
    grid_rows = grid_state.shape[0]
    mesh_rows = mesh_state.shape[0]
    grid_tiles = grid_rows // TILE
    mesh_tiles = mesh_rows // TILE
    all_mesh_tiles = mesh_tiles * lax.axis_size("nodes")
    head_columns = encoder_key.shape[1]
    gathered = turned_gather(
        (
            encoder_query,
            encoder_key,
            encoder_value,
            encoder_output,
            window_query,
            window_key,
            window_value,
            window_output,
            expand_weight,
            shrink_weight,
            decoder_query,
            decoder_key,
            decoder_value,
            decoder_output,
        ),
        "nodes",
        (0, 0, 0, 1, 0, 0, 0, 1, 0, 1, 0, 0, 0, 1),
    )
    grid_full = collect(grid_state, "heads", 1)
    grid_norm = normalize(grid_full)
    grid_key, grid_value, grid_query = local_terms(
        grid_norm, (gathered[1], gathered[2], gathered[10])
    )
    grid_queries = (grid_query * scaling).astype(jnp.bfloat16)
    mesh_full = collect(mesh_state, "heads", 1)
    mesh_norm = normalize(mesh_full)
    (mesh_query,) = local_terms(mesh_norm, (gathered[0],))
    mesh_queries = (mesh_query * scaling).astype(jnp.bfloat16)
    rim_tiles = grid_tiles // 2
    stacked = jnp.stack([grid_key.astype(jnp.bfloat16), grid_value.astype(jnp.bfloat16)])
    padded = with_halo(stacked, (("nodes", 1),), rim_tiles * TILE)
    local_index = encoder_blocks - (position * grid_tiles - rim_tiles)
    key_rows, value_rows = pick_tiles(padded, grid_tiles + 2 * rim_tiles, local_index)
    key_mask = slot_mask(encoder_count, encoder_blocks.shape[1])
    encoded = attend_blocks(
        mesh_queries.reshape(mesh_tiles, TILE, head_columns), key_rows, value_rows, key_mask
    ).reshape(mesh_rows, head_columns)
    (encoder_terms,) = local_terms(encoded, (gathered[3],))
    encoder_pieces = lax.all_to_all(
        encoder_terms.astype(jnp.bfloat16), "heads", split_axis=1, concat_axis=0, tiled=True
    ).astype(encoder_terms.dtype)
    share_one = (mesh_state.astype(jnp.float32) + fold_parts(encoder_pieces, mesh_rows)).astype(
        jnp.bfloat16
    )
    mesh_one = collect(share_one, "heads", 1)
    norm_one = normalize(mesh_one)
    window_queries, window_keys, window_values = local_terms(
        norm_one, (gathered[4], gathered[5], gathered[6])
    )
    window_queries = (window_queries * scaling).astype(jnp.bfloat16)
    stacked = jnp.stack([window_keys.astype(jnp.bfloat16), window_values.astype(jnp.bfloat16)])
    padded = with_halo(stacked, (("nodes", 1),), mesh_rows)
    tile_here = jnp.arange(mesh_tiles, dtype=jnp.int32)[:, None]
    key_rows, value_rows = pick_tiles(
        padded, 3 * mesh_tiles, tile_here + mesh_tiles + window_offsets
    )
    reached = position * mesh_tiles + tile_here + window_offsets
    key_mask = jnp.repeat((reached >= 0) & (reached < all_mesh_tiles), TILE, axis=1)
    windowed = attend_blocks(
        window_queries.reshape(mesh_tiles, TILE, head_columns), key_rows, value_rows, key_mask
    ).reshape(mesh_rows, head_columns)
    (window_terms,) = local_terms(windowed, (gathered[7],))
    window_pieces = lax.all_to_all(
        window_terms.astype(jnp.bfloat16), "heads", split_axis=1, concat_axis=0, tiled=True
    ).astype(window_terms.dtype)
    share_two = (share_one.astype(jnp.float32) + fold_parts(window_pieces, mesh_rows)).astype(
        jnp.bfloat16
    )
    mesh_two = collect(share_two, "heads", 1)
    norm_two = normalize(mesh_two)
    (hidden,) = local_terms(norm_two, (gathered[8],))
    hidden = jax.nn.gelu(hidden, approximate=False).astype(jnp.bfloat16)
    (hidden_terms,) = local_terms(hidden, (gathered[9],))
    hidden_pieces = lax.all_to_all(
        hidden_terms.astype(jnp.bfloat16), "heads", split_axis=1, concat_axis=0, tiled=True
    ).astype(hidden_terms.dtype)
    mesh_out = (share_two.astype(jnp.float32) + fold_parts(hidden_pieces, mesh_rows)).astype(
        jnp.bfloat16
    )
    mesh_three = collect(mesh_out, "heads", 1)
    norm_three = normalize(mesh_three)
    mesh_keys, mesh_values = local_terms(norm_three, (gathered[11], gathered[12]))
    stacked = jnp.stack([mesh_keys.astype(jnp.bfloat16), mesh_values.astype(jnp.bfloat16)])
    padded = with_halo(stacked, (("nodes", 1),), TILE)
    local_index = decoder_blocks - (position * mesh_tiles - 1)
    key_rows, value_rows = pick_tiles(padded, mesh_tiles + 2, local_index)
    key_mask = slot_mask(decoder_count, decoder_blocks.shape[1])
    decoded = attend_blocks(
        grid_queries.reshape(grid_tiles, TILE, head_columns), key_rows, value_rows, key_mask
    ).reshape(grid_rows, head_columns)
    (decoder_terms,) = local_terms(decoded, (gathered[13],))
    decoder_share = sum_at_owner(decoder_terms.astype(jnp.bfloat16), "heads", 1)
    grid_out = (grid_state.astype(jnp.float32) + decoder_share).astype(jnp.bfloat16)
    return (grid_out, mesh_out)


def solution(mesh):
    in_specs = (
        P("nodes", "heads"),
        P("nodes", "heads"),
        P("nodes", "heads"),
        P("nodes", "heads"),
        P("nodes", "heads"),
        P("heads", "nodes"),
        P("nodes", "heads"),
        P("nodes", "heads"),
        P("nodes", "heads"),
        P("heads", "nodes"),
        P("nodes", "heads"),
        P("heads", "nodes"),
        P("nodes", "heads"),
        P("nodes", "heads"),
        P("nodes", "heads"),
        P("heads", "nodes"),
        P("nodes", None),
        P("nodes"),
        P("nodes", None),
        P("nodes", None),
        P("nodes"),
    )
    out_specs = (P("nodes", "heads"), P("nodes", "heads"))
    return jax.shard_map(local, mesh=mesh, in_specs=in_specs, out_specs=out_specs, check_vma=False)
```

profile of v0, /device:TPU:31, one launch (start us, length us, event | category | flops | bytes accessed | tf_op | source)
XLA Modules:
  0.0 417.6 jit_solution(11510416851069582192)
XLA Ops:
  17.6 1.0 copy.55
  19.4 5.6 %all-to-all-start.1 = ((bf16[4,256,256]{1,2,0:T(8,128)(2,1)}), bf16[4,256,256]{1,2,0:T(8,128)(2,1)S(1)}, u32[]{:S(2)}, u32[]{:S(2)}) async-start(bf16[4,256,256]{1,2,0:T(8,128)(2,1)} %broadcast_in_dim.174), calls=%async_computation.1 | async-start | bytes 1048576 | tf_op jit(solution)/shard_map/all_to_all | solution.py:34
  25.2 13.8 %all-to-all-done.1 = bf16[4,256,256]{1,2,0:T(8,128)(2,1)S(1)} async-done(((bf16[4,256,256]{1,2,0:T(8,128)(2,1)}), bf16[4,256,256]{1,2,0:T(8,128)(2,1)S(1)}, u32[]{:S(2)}, u32[]{:S(2)}) %all-to-all-start.1) | async-done | bytes 524320 | tf_op jit(solution)/shard_map/all_to_all | solution.py:34
  39.1 1.6 broadcast_in_dim.168
  40.7 3.7 all-to-all-start
  45.1 53.9 %all-to-all-done = bf16[4,1024,256]{1,2,0:T(8,128)(2,1)S(1)} async-done(((bf16[4,1024,256]{1,2,0:T(8,128)(2,1)}), bf16[4,1024,256]{1,2,0:T(8,128)(2,1)S(1)}, u32[]{:S(2)}, u32[]{:S(2)}) %all-to-all-start) | async-done | bytes 2097184 | tf_op jit(solution)/shard_map/all_to_all | solution.py:34
  100.0 2.0 fusion.8
  102.0 61.1 %all-gather.2.cloned.1.call-done = bf16[1024,2560]{1,0:T(8,128)(2,1)} async-done(((bf16[8,2560]{1,0:T(8,128)(2,1)}), bf16[1024,2560]{1,0:T(8,128)(2,1)}) %all-gather.2.cloned.1.call-update) | async-done | bytes 5242896 | tf_op jit(solution)/shard_map/all_gather | solution.py:16
  163.1 2.4 fusion.14
  165.4 1.7 fusion.13
  167.2 4.0 collective-permute-start
  171.2 1.9 collective-permute-start.1
  173.3 1.3 fusion.15
  174.7 19.8 %collective-permute-done.1 = bf16[2,512,128]{2,1,0:T(8,128)(2,1)S(1)} collective-permute-done((bf16[2,512,128]{2,1,0:T(8,128)(2,1)S(1)}, bf16[2,512,128]{2,1,0:T(8,128)(2,1)S(1)}, u32[]{:S(2)}, u32[]{:S(2)}) %collective-permute-start.1) | collective-permute-done | bytes 262176 | tf_op jit(solution)/shard_map/ppermute | solution.py:49
  194.5 1.0 pad_maximum_fusion
  198.4 1.2 fusion.17
  199.7 1.3 convolution_convert_fusion.4
  201.0 14.9 %all_to_all.69 = bf16[256,4,256]{2,0,1:T(8,128)(2,1)S(1)} all-to-all(bf16[256,4,256]{2,0,1:T(8,128)(2,1)S(1)} %bitcast.190), channel_id=1, replica_groups=mesh['nodes'=128,'heads'=4] {'heads'}, dimensions={1} | all-to-all | bytes 1048576 | tf_op jit(solution)/shard_map/all_to_all | solution.py:203
  217.0 3.5 all-to-all-start.3
  220.7 8.8 %all-to-all-done.3 = bf16[4,256,256]{1,2,0:T(8,128)(2,1)S(1)} async-done(((bf16[4,256,256]{1,2,0:T(8,128)(2,1)}), bf16[4,256,256]{1,2,0:T(8,128)(2,1)S(1)}, u32[]{:S(2)}, u32[]{:S(2)}) %all-to-all-start.3) | async-done | bytes 524320 | tf_op jit(solution)/shard_map/all_to_all | solution.py:34
  230.1 1.3 fusion.19
  231.4 1.3 fusion.18
  232.7 1.9 collective-permute-start.3
  234.6 11.9 %collective-permute-start.2 = (bf16[2,256,128]{2,1,0:T(8,128)(2,1)S(1)}, bf16[2,256,128]{2,1,0:T(8,128)(2,1)S(1)}, u32[]{:S(2)}, u32[]{:S(2)}) collective-permute-start(bf16[2,256,128]{2,1,0:T(8,128)(2,1)S(1)} %pad_maximum_fusion.4), channel_id=1, source_target_pairs={{0,4},{4,8},{8,12},{12,16},{16,20},{20,24},{24,28},{28,32},{32,36}... | collective-permute-start | bytes 393224 | tf_op jit(solution)/shard_map/ppermute | solution.py:48
  246.6 1.3 fusion.16
  248.0 2.9 collective-permute-done.3
  253.3 1.1 fusion.20
  254.5 1.3 convolution_convert_fusion.3
  255.8 17.0 %all_to_all.70 = bf16[256,4,256]{2,0,1:T(8,128)(2,1)S(1)} all-to-all(bf16[256,4,256]{2,0,1:T(8,128)(2,1)S(1)} %bitcast.192), channel_id=1, replica_groups=mesh['nodes'=128,'heads'=4] {'heads'}, dimensions={1} | all-to-all | bytes 1048576 | tf_op jit(solution)/shard_map/all_to_all | solution.py:227
  273.0 12.2 %all_to_all.71 = bf16[4,256,256]{1,2,0:T(8,128)(2,1)S(1)} all-to-all(bf16[4,256,256]{1,2,0:T(8,128)(2,1)S(1)} %broadcast_in_dim.184), channel_id=1, replica_groups=mesh['nodes'=128,'heads'=4] {'heads'}, dimensions={0} | all-to-all | bytes 1048576 | tf_op jit(solution)/shard_map/all_to_all | solution.py:34
  285.8 3.5 convolution_convert_fusion.2
  289.3 14.7 %all_to_all.72 = bf16[256,4,256]{2,0,1:T(8,128)(2,1)S(1)} all-to-all(bf16[256,4,256]{2,0,1:T(8,128)(2,1)S(1)} %bitcast.193), channel_id=1, replica_groups=mesh['nodes'=128,'heads'=4] {'heads'}, dimensions={1} | all-to-all | bytes 1048576 | tf_op jit(solution)/shard_map/all_to_all | solution.py:238
  305.0 4.7 %all-to-all-start.7 = ((bf16[4,256,256]{1,2,0:T(8,128)(2,1)}), bf16[4,256,256]{1,2,0:T(8,128)(2,1)S(1)}, u32[]{:S(2)}, u32[]{:S(2)}) async-start(bf16[4,256,256]{1,2,0:T(8,128)(2,1)} %broadcast_in_dim.185), calls=%async_computation.7 | async-start | bytes 1048576 | tf_op jit(solution)/shard_map/all_to_all | solution.py:34
  310.2 8.7 %all-to-all-done.7 = bf16[4,256,256]{1,2,0:T(8,128)(2,1)S(1)} async-done(((bf16[4,256,256]{1,2,0:T(8,128)(2,1)}), bf16[4,256,256]{1,2,0:T(8,128)(2,1)S(1)}, u32[]{:S(2)}, u32[]{:S(2)}) %all-to-all-start.7) | async-done | bytes 524320 | tf_op jit(solution)/shard_map/all_to_all | solution.py:34
  319.4 1.3 fusion.22
  320.7 1.3 fusion.21
  322.0 17.6 %collective-permute-start.4 = (bf16[2,128,128]{2,1,0:T(8,128)(2,1)S(1)}, bf16[2,128,128]{2,1,0:T(8,128)(2,1)S(1)}, u32[]{:S(2)}, u32[]{:S(2)}) collective-permute-start(bf16[2,128,128]{2,1,0:T(8,128)(2,1)S(1)} %get-tuple-element.121), channel_id=1, source_target_pairs={{0,4},{4,8},{8,12},{12,16},{16,20},{20,24},{24,28},{28,32},{32,36}... | collective-permute-start | bytes 196616 | tf_op jit(solution)/shard_map/ppermute | solution.py:48
  339.6 1.9 collective-permute-start.5
  341.5 1.7 fusion.12
  343.2 12.3 %collective-permute-done.5 = bf16[2,128,128]{2,1,0:T(8,128)(2,1)S(1)} collective-permute-done((bf16[2,128,128]{2,1,0:T(8,128)(2,1)S(1)}, bf16[2,128,128]{2,1,0:T(8,128)(2,1)S(1)}, u32[]{:S(2)}, u32[]{:S(2)}) %collective-permute-start.5) | collective-permute-done | bytes 65568 | tf_op jit(solution)/shard_map/ppermute | solution.py:49
  356.9 12.0 %while.2 = (s32[]{:T(128)}, bf16[2,4,128,128]{3,2,1,0:T(8,128)(2,1)}, bf16[2,4,384,128]{3,2,1,0:T(8,128)(2,1)S(1)}, pred[2,4,384]{2,1,0:T(4,128)(4,1)S(1)}, bf16...) while((s32[]{:T(128)}, bf16[2,4,128,128]{3,2,1,0:T(8,128)(2,1)}, ...), condition=%wide.region_20.21_spmd, body=%wide.region_17.20_spmd.sunk | while | flops 102695296 | bytes 12595925 | solution.py:116
  358.1 1.9 fusion.191
  360.0 2.0 convolution_convert_fusion.14
  364.1 1.9 fusion.191
  366.0 2.0 convolution_convert_fusion.14
  368.9 1.7 convolution_convert_fusion.1
  370.6 38.6 %all_to_all.73 = bf16[4,1024,256]{1,2,0:T(8,128)(2,1)S(1)} all-to-all(bf16[4,1024,256]{1,2,0:T(8,128)(2,1)S(1)} %bitcast.181), channel_id=1, replica_groups=mesh['nodes'=128,'heads'=4] {'heads'}, dimensions={0} | all-to-all | bytes 4194304 | tf_op jit(solution)/shard_map/all_to_all | solution.py:61
  409.8 1.0 copy.75
  (167 shorter events, 29.4 us)
Async XLA Ops:
  7.2 17.9 %copy-start.5 = (bf16[1024,256]{1,0:T(8,128)(2,1)S(1)}, bf16[1024,256]{1,0:T(8,128)(2,1)}, u32[]{:S(2)}) copy-start(bf16[1024,256]{1,0:T(8,128)(2,1)} %param.23) | copy-start | bytes 1572868
  7.2 155.9 %all-gather.2.cloned.1.call-start = ((), (), s32[]{:S(2)}) async-start(), calls=%async_computation.9 | async-start | bytes 5283840 | tf_op jit(solution)/shard_map/all_gather | solution.py:16
  16.9 0.6 copy-start.10
  19.4 19.7 %all-to-all-start.1 = ((bf16[4,256,256]{1,2,0:T(8,128)(2,1)}), bf16[4,256,256]{1,2,0:T(8,128)(2,1)S(1)}, u32[]{:S(2)}, u32[]{:S(2)}) async-start(bf16[4,256,256]{1,2,0:T(8,128)(2,1)} %broadcast_in_dim.174), calls=%async_computation.1 | async-start | bytes 1048576 | tf_op jit(solution)/shard_map/all_to_all | solution.py:34
  40.7 3.8 copy-start.12
  40.7 3.9 copy-start.14
  40.7 58.3 %all-to-all-start = ((bf16[4,1024,256]{1,2,0:T(8,128)(2,1)}), bf16[4,1024,256]{1,2,0:T(8,128)(2,1)S(1)}, u32[]{:S(2)}, u32[]{:S(2)}) async-start(bf16[4,1024,256]{1,2,0:T(8,128)(2,1)} %broadcast_in_dim.168), calls=%async_computation | async-start | bytes 4194304 | tf_op jit(solution)/shard_map/all_to_all | solution.py:34
  102.0 63.5 %copy-start = (bf16[1024,1024]{0,1:T(8,128)(2,1)S(1)}, bf16[1024,1024]{0,1:T(8,128)(2,1)}, u32[]{:S(2)}) copy-start(bf16[1024,1024]{0,1:T(8,128)(2,1)} %fusion.8) | copy-start | bytes 6291460
  167.2 6.1 %copy-start.4 = (bf16[1,1024,128]{2,1,0:T(8,128)(2,1)}, bf16[1,1024,128]{2,1,0:T(8,128)(2,1)S(1)}, u32[]{:S(2)}) copy-start(bf16[1,1024,128]{2,1,0:T(8,128)(2,1)S(1)} %fusion.13) | copy-start | bytes 786436
  167.2 7.4 %collective-permute-start = (bf16[2,512,128]{2,1,0:T(8,128)(2,1)S(1)}, bf16[2,512,128]{2,1,0:T(8,128)(2,1)S(1)}, u32[]{:S(2)}, u32[]{:S(2)}) collective-permute-start(bf16[2,512,128]{2,1,0:T(8,128)(2,1)S(1)} %get-tuple-element.119), channel_id=1, source_target_pairs={{0,4},{4,8},{8,12},{12,16},{16,20},{20,24},{24,28},{28,32},{32,36}... | collective-permute-start | bytes 786440 | tf_op jit(solution)/shard_map/ppermute | solution.py:48
  171.2 23.3 %collective-permute-start.1 = (bf16[2,512,128]{2,1,0:T(8,128)(2,1)S(1)}, bf16[2,512,128]{2,1,0:T(8,128)(2,1)S(1)}, u32[]{:S(2)}, u32[]{:S(2)}) collective-permute-start(bf16[2,512,128]{2,1,0:T(8,128)(2,1)S(1)} %get-tuple-element.120), channel_id=1, source_target_pairs={{4,0},{8,4},{12,8},{16,12},{20,16},{24,20},{28,24},{32,28},{36,32}... | collective-permute-start | bytes 786440 | tf_op jit(solution)/shard_map/ppermute | solution.py:49
  199.6 16.4 %copy-start.6 = (bf16[256,256]{1,0:T(8,128)(2,1)S(1)}, bf16[256,256]{1,0:T(8,128)(2,1)}, u32[]{:S(2)}) copy-start(bf16[256,256]{1,0:T(8,128)(2,1)} %param.24) | copy-start | bytes 393220
  201.0 19.4 %copy-start.13 = (s32[2,4]{1,0:T(2,128)S(1)}, s32[2,4]{1,0:T(2,128)}, u32[]{:S(2)}) copy-start(s32[2,4]{1,0:T(2,128)} %param.41) | copy-start | bytes 100
  217.0 12.6 %all-to-all-start.3 = ((bf16[4,256,256]{1,2,0:T(8,128)(2,1)}), bf16[4,256,256]{1,2,0:T(8,128)(2,1)S(1)}, u32[]{:S(2)}, u32[]{:S(2)}) async-start(bf16[4,256,256]{1,2,0:T(8,128)(2,1)} %broadcast_in_dim.177), calls=%async_computation.3 | async-start | bytes 1048576 | tf_op jit(solution)/shard_map/all_to_all | solution.py:34
  232.7 18.2 %collective-permute-start.3 = (bf16[2,256,128]{2,1,0:T(8,128)(2,1)S(1)}, bf16[2,256,128]{2,1,0:T(8,128)(2,1)S(1)}, u32[]{:S(2)}, u32[]{:S(2)}) collective-permute-start(bf16[2,256,128]{2,1,0:T(8,128)(2,1)S(1)} %pad_maximum_fusion.4), channel_id=1, source_target_pairs={{4,0},{8,4},{12,8},{16,12},{20,16},{24,20},{28,24},{32,28},{36,32}... | collective-permute-start | bytes 393224 | tf_op jit(solution)/shard_map/ppermute | solution.py:49
  234.6 16.2 %collective-permute-start.2 = (bf16[2,256,128]{2,1,0:T(8,128)(2,1)S(1)}, bf16[2,256,128]{2,1,0:T(8,128)(2,1)S(1)}, u32[]{:S(2)}, u32[]{:S(2)}) collective-permute-start(bf16[2,256,128]{2,1,0:T(8,128)(2,1)S(1)} %pad_maximum_fusion.4), channel_id=1, source_target_pairs={{0,4},{4,8},{8,12},{12,16},{16,20},{20,24},{24,28},{28,32},{32,36}... | collective-permute-start | bytes 393224 | tf_op jit(solution)/shard_map/ppermute | solution.py:48
  289.3 20.5 %copy-start.11 = (s32[8,3]{0,1:T(4,128)S(1)}, s32[8,3]{0,1:T(4,128)}, u32[]{:S(2)}) copy-start(s32[8,3]{0,1:T(4,128)} %param.42) | copy-start | bytes 292
  289.3 20.6 %copy-start.15 = (s32[8]{0:T(128)S(1)}, s32[8]{0:T(128)}, u32[]{:S(2)}) copy-start(s32[8]{0:T(128)} %param.43) | copy-start | bytes 100
  304.1 16.6 %copy-start.7 = (bf16[256,256]{1,0:T(8,128)(2,1)}, bf16[256,256]{1,0:T(8,128)(2,1)S(1)}, u32[]{:S(2)}) copy-start(bf16[256,256]{1,0:T(8,128)(2,1)S(1)} %add_convert_fusion.1) | copy-start | bytes 393220
  305.0 13.8 %all-to-all-start.7 = ((bf16[4,256,256]{1,2,0:T(8,128)(2,1)}), bf16[4,256,256]{1,2,0:T(8,128)(2,1)S(1)}, u32[]{:S(2)}, u32[]{:S(2)}) async-start(bf16[4,256,256]{1,2,0:T(8,128)(2,1)} %broadcast_in_dim.185), calls=%async_computation.7 | async-start | bytes 1048576 | tf_op jit(solution)/shard_map/all_to_all | solution.py:34
  309.7 31.8 %copy-start.1 = (bf16[1024,1024]{0,1:T(8,128)(2,1)S(1)}, bf16[1024,1024]{0,1:T(8,128)(2,1)}, u32[]{:S(2)}) copy-start(bf16[1024,1024]{0,1:T(8,128)(2,1)} %fusion.8) | copy-start | bytes 6291460
  322.0 21.2 %collective-permute-start.4 = (bf16[2,128,128]{2,1,0:T(8,128)(2,1)S(1)}, bf16[2,128,128]{2,1,0:T(8,128)(2,1)S(1)}, u32[]{:S(2)}, u32[]{:S(2)}) collective-permute-start(bf16[2,128,128]{2,1,0:T(8,128)(2,1)S(1)} %get-tuple-element.121), channel_id=1, source_target_pairs={{0,4},{4,8},{8,12},{12,16},{16,20},{20,24},{24,28},{28,32},{32,36}... | collective-permute-start | bytes 196616 | tf_op jit(solution)/shard_map/ppermute | solution.py:48
  339.6 16.0 %collective-permute-start.5 = (bf16[2,128,128]{2,1,0:T(8,128)(2,1)S(1)}, bf16[2,128,128]{2,1,0:T(8,128)(2,1)S(1)}, u32[]{:S(2)}, u32[]{:S(2)}) collective-permute-start(bf16[2,128,128]{2,1,0:T(8,128)(2,1)S(1)} %get-tuple-element.122), channel_id=1, source_target_pairs={{4,0},{8,4},{12,8},{16,12},{20,16},{24,20},{28,24},{32,28},{36,32}... | collective-permute-start | bytes 196616 | tf_op jit(solution)/shard_map/ppermute | solution.py:49
  356.9 0.7 copy-start.2
  360.0 2.2 copy-start.8
  360.0 2.9 copy-start.3
  362.2 0.7 copy-start.9
  362.9 0.7 copy-start.2
  366.0 2.2 copy-start.8
  366.0 2.9 copy-start.3
  368.2 0.7 copy-start.9
Sparse Core Ops, SparseCore 0:
  17.7 145.3 all-gather.1
where the time goes:
time: 419 us; the launch traced here: 418 us
  waiting for transfers between devices  181 us (43%)
  blocking collectives  97.4 us (23%)
  starting transfers between devices  56.8 us (14%)
  matrix products  32.7 us (8%)
  local copies, waits for them, and re-layouts  26.6 us (6%)
  between operations  14.7 us (4%)
  other arithmetic  7.87 us (2%)
    all_to_all x4, waiting for transfers between devices, from_everyone(): lax.all_to_all(jnp.broadcast_to(x[None], (length, *x.shape)), axis, 0, 0,...  85.2 us
    all_gather x1, waiting for transfers between devices, turned_gather(): whole = lax.all_gather(both, axis, axis=0, tiled=True)  61.1 us
    all_to_all x1, blocking collectives, sum_at_owner(): lax.all_to_all(parts, axis, split_axis=0, concat_axis=0, tiled=True)  38.6 us
    ppermute x3, waiting for transfers between devices, with_halo(): after = lax.ppermute(first, axis, down)  35 us
    ppermute x3, starting transfers between devices, with_halo(): before = lax.ppermute(last, axis, up)  33.5 us
    dot_general x13, matrix products, local_terms(): jnp.dot(source, member, preferred_element_type=jnp.float32)  21.2 us
    all_to_all x4, starting transfers between devices, from_everyone(): lax.all_to_all(jnp.broadcast_to(x[None], (length, *x.shape)), axis, 0, 0,...  17.5 us
    all_to_all x1, blocking collectives, local(): lax.all_to_all(window_terms.astype(jnp.bfloat16), 'heads', split_axis=1,...  17 us
  transfers between devices with their start and end apart: 11, of which 8 were waited for; matrix products, arithmetic and copies ran while one was open for 3% of the time, Pallas kernels for 0%

commit v1 on v0

--- a/solution.py
+++ b/solution.py
@@ -13,7 +13,9 @@
     turned = [jnp.moveaxis(a, dim, 0) for a, dim in zip(arrays, dims)]
     widths = [t[0].size for t in turned]
     both = jnp.concatenate([t.reshape(-1, w) for t, w in zip(turned, widths)], axis=1)
-    whole = lax.all_gather(both, axis, axis=0, tiled=True)
+    whole = jnp.concatenate(
+        lax.all_to_all(jnp.stack([both] * lax.axis_size(axis)), axis, 0, 0), axis=0
+    )
     parts = jnp.split(whole, [sum(widths[:k]) for k in range(1, len(widths))], axis=1)
     return tuple(
         (

time: 419 us -> 568 us (1.36)
  the two profiles are of different devices: /device:TPU:31 before, /device:TPU:128 now
where the time goes in v1:
time: 568 us; the launch traced here: 567 us
  waiting for transfers between devices  341 us (60%)
  blocking collectives  112 us (20%)
  starting transfers between devices  54.4 us (10%)
  matrix products  32.9 us (6%)
  local copies, waits for them, and re-layouts  18.6 us (3%)
  other arithmetic  6.85 us (1%)
    all_to_all x1, waiting for transfers between devices, turned_gather(): lax.all_to_all(jnp.stack([both] * lax.axis_size(axis)), axis, 0, 0)  226 us
    all_to_all x4, waiting for transfers between devices, from_everyone(): lax.all_to_all(jnp.broadcast_to(x[None], (length, *x.shape)), axis, 0, 0,...  81.2 us
    all_to_all x1, blocking collectives, sum_at_owner(): lax.all_to_all(parts, axis, split_axis=0, concat_axis=0, tiled=True)  41.8 us
    ppermute x3, waiting for transfers between devices, with_halo(): before = lax.ppermute(last, axis, up)  28.6 us
    dot_general x13, matrix products, local_terms(): jnp.dot(source, member, preferred_element_type=jnp.float32)  21.4 us
    all_to_all x1, starting transfers between devices, turned_gather(): lax.all_to_all(jnp.stack([both] * lax.axis_size(axis)), axis, 0, 0)  18.7 us
    all_to_all x1, blocking collectives, local(): lax.all_to_all(encoder_terms.astype(jnp.bfloat16), 'heads', split_axis=1,...  18.6 us
    all_to_all x1, blocking collectives, local(): lax.all_to_all(window_terms.astype(jnp.bfloat16), 'heads', split_axis=1,...  17.6 us
  transfers between devices with their start and end apart: 11, of which 10 were waited for; matrix products, arithmetic and copies ran while one was open for 2% of the time, Pallas kernels for 0%

profile of v1, /device:TPU:128, one launch (start us, length us, event | category | flops | bytes accessed | tf_op | source)
XLA Modules:
  0.0 567.0 jit_solution(16983626604767132267)
XLA Ops:
  2.5 5.9 %all-to-all-start.2 = ((bf16[4,256,256]{1,2,0:T(8,128)(2,1)}), bf16[4,256,256]{1,2,0:T(8,128)(2,1)S(1)}, u32[]{:S(2)}, u32[]{:S(2)}) async-start(bf16[4,256,256]{1,2,0:T(8,128)(2,1)} %broadcast_in_dim.174), calls=%async_computation.2 | async-start | bytes 1048576 | tf_op jit(solution)/shard_map/all_to_all | solution.py:36
  8.6 14.3 %all-to-all-done.2 = bf16[4,256,256]{1,2,0:T(8,128)(2,1)S(1)} async-done(((bf16[4,256,256]{1,2,0:T(8,128)(2,1)}), bf16[4,256,256]{1,2,0:T(8,128)(2,1)S(1)}, u32[]{:S(2)}, u32[]{:S(2)}) %all-to-all-start.2) | async-done | bytes 524320 | tf_op jit(solution)/shard_map/all_to_all | solution.py:36
  22.9 1.6 broadcast_in_dim.168
  24.7 3.8 all-to-all-start
  28.7 47.4 %all-to-all-done = bf16[4,1024,256]{1,2,0:T(8,128)(2,1)S(1)} async-done(((bf16[4,1024,256]{1,2,0:T(8,128)(2,1)}), bf16[4,1024,256]{1,2,0:T(8,128)(2,1)S(1)}, u32[]{:S(2)}, u32[]{:S(2)}) %all-to-all-start) | async-done | bytes 2097184 | tf_op jit(solution)/shard_map/all_to_all | solution.py:36
  76.2 2.7 stack.20
  78.8 18.7 %all-to-all-start.1 = ((bf16[128,8,2560]{2,1,0:T(8,128)(2,1)}), bf16[128,8,2560]{2,1,0:T(8,128)(2,1)}, u32[]{:S(2)}, u32[]{:S(2)}) async-start(bf16[128,8,2560]{2,1,0:T(8,128)(2,1)} %stack.20), calls=%async_computation.1 | async-start | bytes 10485760 | tf_op jit(solution)/shard_map/all_to_all | solution.py:17
  99.2 1.9 fusion.8
  101.1 225.8 %all-to-all-done.1 = bf16[128,8,2560]{2,1,0:T(8,128)(2,1)} async-done(((bf16[128,8,2560]{2,1,0:T(8,128)(2,1)}), bf16[128,8,2560]{2,1,0:T(8,128)(2,1)}, u32[]{:S(2)}, u32[]{:S(2)}) %all-to-all-start.1) | async-done | bytes 5242912 | tf_op jit(solution)/shard_map/all_to_all | solution.py:17
  326.9 2.5 fusion.13
  329.4 1.7 fusion.14
  331.2 8.2 %collective-permute-start.1 = (bf16[2,512,128]{2,1,0:T(8,128)(2,1)S(1)}, bf16[2,512,128]{2,1,0:T(8,128)(2,1)S(1)}, u32[]{:S(2)}, u32[]{:S(2)}) collective-permute-start(bf16[2,512,128]{2,1,0:T(8,128)(2,1)S(1)} %get-tuple-element.120), channel_id=1, source_target_pairs={{4,0},{8,4},{12,8},{16,12},{20,16},{24,20},{28,24},{32,28},{36,32}... | collective-permute-start | bytes 786440 | tf_op jit(solution)/shard_map/ppermute | solution.py:51
  339.4 1.9 collective-permute-start
  341.4 1.3 fusion.15
  342.8 3.2 collective-permute-done.1
  346.1 9.2 %collective-permute-done = bf16[2,512,128]{2,1,0:T(8,128)(2,1)S(1)} collective-permute-done((bf16[2,512,128]{2,1,0:T(8,128)(2,1)S(1)}, bf16[2,512,128]{2,1,0:T(8,128)(2,1)S(1)}, u32[]{:S(2)}, u32[]{:S(2)}) %collective-permute-start) | collective-permute-done | bytes 262176 | tf_op jit(solution)/shard_map/ppermute | solution.py:50
  358.3 1.2 fusion.17
  359.6 1.3 convolution_convert_fusion.4
  360.9 18.6 %all_to_all.74 = bf16[256,4,256]{2,0,1:T(8,128)(2,1)S(1)} all-to-all(bf16[256,4,256]{2,0,1:T(8,128)(2,1)S(1)} %bitcast.191), channel_id=1, replica_groups=mesh['nodes'=128,'heads'=4] {'heads'}, dimensions={1} | all-to-all | bytes 1048576 | tf_op jit(solution)/shard_map/all_to_all | solution.py:205
  380.6 3.7 all-to-all-start.4
  384.5 9.8 %all-to-all-done.4 = bf16[4,256,256]{1,2,0:T(8,128)(2,1)S(1)} async-done(((bf16[4,256,256]{1,2,0:T(8,128)(2,1)}), bf16[4,256,256]{1,2,0:T(8,128)(2,1)S(1)}, u32[]{:S(2)}, u32[]{:S(2)}) %all-to-all-start.4) | async-done | bytes 524320 | tf_op jit(solution)/shard_map/all_to_all | solution.py:36
  394.9 1.3 fusion.19
  396.1 1.3 fusion.18
  397.5 1.9 collective-permute-start.3
  399.4 2.4 collective-permute-start.2
  401.8 1.3 fusion.16
  403.2 2.0 collective-permute-done.3
  405.2 10.0 %collective-permute-done.2 = bf16[2,256,128]{2,1,0:T(8,128)(2,1)S(1)} collective-permute-done((bf16[2,256,128]{2,1,0:T(8,128)(2,1)S(1)}, bf16[2,256,128]{2,1,0:T(8,128)(2,1)S(1)}, u32[]{:S(2)}, u32[]{:S(2)}) %collective-permute-start.2) | collective-permute-done | bytes 131104 | tf_op jit(solution)/shard_map/ppermute | solution.py:50
  418.8 1.3 convolution_convert_fusion.3
  420.1 17.6 %all_to_all.75 = bf16[256,4,256]{2,0,1:T(8,128)(2,1)S(1)} all-to-all(bf16[256,4,256]{2,0,1:T(8,128)(2,1)S(1)} %bitcast.193), channel_id=1, replica_groups=mesh['nodes'=128,'heads'=4] {'heads'}, dimensions={1} | all-to-all | bytes 1048576 | tf_op jit(solution)/shard_map/all_to_all | solution.py:229
  438.1 17.4 %all_to_all.76 = bf16[4,256,256]{1,2,0:T(8,128)(2,1)S(1)} all-to-all(bf16[4,256,256]{1,2,0:T(8,128)(2,1)S(1)} %broadcast_in_dim.184), channel_id=1, replica_groups=mesh['nodes'=128,'heads'=4] {'heads'}, dimensions={0} | all-to-all | bytes 1048576 | tf_op jit(solution)/shard_map/all_to_all | solution.py:36
  456.0 3.5 convolution_convert_fusion.2
  459.6 16.2 %all_to_all.77 = bf16[256,4,256]{2,0,1:T(8,128)(2,1)S(1)} all-to-all(bf16[256,4,256]{2,0,1:T(8,128)(2,1)S(1)} %bitcast.194), channel_id=1, replica_groups=mesh['nodes'=128,'heads'=4] {'heads'}, dimensions={1} | all-to-all | bytes 1048576 | tf_op jit(solution)/shard_map/all_to_all | solution.py:240
  476.8 3.5 all-to-all-start.8
  480.8 9.8 %all-to-all-done.8 = bf16[4,256,256]{1,2,0:T(8,128)(2,1)S(1)} async-done(((bf16[4,256,256]{1,2,0:T(8,128)(2,1)}), bf16[4,256,256]{1,2,0:T(8,128)(2,1)S(1)}, u32[]{:S(2)}, u32[]{:S(2)}) %all-to-all-start.8) | async-done | bytes 524320 | tf_op jit(solution)/shard_map/all_to_all | solution.py:36
  491.0 1.3 fusion.21
  492.3 1.3 fusion.22
  493.6 1.9 collective-permute-start.5
  495.6 2.6 collective-permute-start.4
  498.2 1.7 fusion.12
  499.9 9.3 %collective-permute-done.4 = bf16[2,128,128]{2,1,0:T(8,128)(2,1)S(1)} collective-permute-done((bf16[2,128,128]{2,1,0:T(8,128)(2,1)S(1)}, bf16[2,128,128]{2,1,0:T(8,128)(2,1)S(1)}, u32[]{:S(2)}, u32[]{:S(2)}) %collective-permute-start.4) | collective-permute-done | bytes 65568 | tf_op jit(solution)/shard_map/ppermute | solution.py:50
  510.6 11.2 %while.2 = (s32[]{:T(128)}, bf16[2,4,128,128]{3,2,1,0:T(8,128)(2,1)}, bf16[2,4,384,128]{3,2,1,0:T(8,128)(2,1)S(1)}, pred[2,4,384]{2,1,0:T(4,128)(4,1)S(1)}, bf16...) while((s32[]{:T(128)}, bf16[2,4,128,128]{3,2,1,0:T(8,128)(2,1)}, ...), condition=%wide.region_20.21_spmd, body=%wide.region_17.20_spmd.sunk | while | flops 102695296 | bytes 10498717 | solution.py:118
  511.6 1.9 fusion.191
  513.4 2.0 convolution_convert_fusion.14
  517.2 1.9 fusion.191
  519.0 2.0 convolution_convert_fusion.14
  521.9 1.7 convolution_convert_fusion.1
  523.6 41.8 %all_to_all.78 = bf16[4,1024,256]{1,2,0:T(8,128)(2,1)S(1)} all-to-all(bf16[4,1024,256]{1,2,0:T(8,128)(2,1)S(1)} %bitcast.182), channel_id=1, replica_groups=mesh['nodes'=128,'heads'=4] {'heads'}, dimensions={0} | all-to-all | bytes 4194304 | tf_op jit(solution)/shard_map/all_to_all | solution.py:63
  (183 shorter events, 21.8 us)
Async XLA Ops:
  0.6 7.8 %copy-start.4 = (bf16[1024,256]{1,0:T(8,128)(2,1)S(1)}, bf16[1024,256]{1,0:T(8,128)(2,1)}, u32[]{:S(2)}) copy-start(bf16[1024,256]{1,0:T(8,128)(2,1)} %param.23) | copy-start | bytes 1572868
  2.5 20.4 %all-to-all-start.2 = ((bf16[4,256,256]{1,2,0:T(8,128)(2,1)}), bf16[4,256,256]{1,2,0:T(8,128)(2,1)S(1)}, u32[]{:S(2)}, u32[]{:S(2)}) async-start(bf16[4,256,256]{1,2,0:T(8,128)(2,1)} %broadcast_in_dim.174), calls=%async_computation.2 | async-start | bytes 1048576 | tf_op jit(solution)/shard_map/all_to_all | solution.py:36
  24.5 3.9 copy-start.9
  24.5 3.9 copy-start.10
  24.5 3.9 copy-start.11
  24.5 4.0 copy-start.12
  24.6 4.0 copy-start.13
  24.6 4.0 copy-start.14
  24.6 4.0 copy-start.15
  24.6 4.0 copy-start.16
  24.6 4.0 copy-start.7
  24.6 4.0 copy-start.8
  24.6 4.0 copy-start.17
  24.6 4.0 copy-start.18
  24.6 4.0 copy-start.19
  24.7 4.1 copy-start.20
  24.7 51.5 %all-to-all-start = ((bf16[4,1024,256]{1,2,0:T(8,128)(2,1)}), bf16[4,1024,256]{1,2,0:T(8,128)(2,1)S(1)}, u32[]{:S(2)}, u32[]{:S(2)}) async-start(bf16[4,1024,256]{1,2,0:T(8,128)(2,1)} %broadcast_in_dim.168), calls=%async_computation | async-start | bytes 4194304 | tf_op jit(solution)/shard_map/all_to_all | solution.py:36
  78.8 18.7 %copy-start.22 = (s32[2,8]{1,0:T(2,128)S(1)}, s32[2,8]{1,0:T(2,128)}, u32[]{:S(2)}) copy-start(s32[2,8]{1,0:T(2,128)} %param.39) | copy-start | bytes 196
  78.8 18.8 %copy-start.24 = (s32[2]{0:T(128)S(1)}, s32[2]{0:T(128)}, u32[]{:S(2)}) copy-start(s32[2]{0:T(128)} %param.40) | copy-start | bytes 28
  78.8 248.1 %all-to-all-start.1 = ((bf16[128,8,2560]{2,1,0:T(8,128)(2,1)}), bf16[128,8,2560]{2,1,0:T(8,128)(2,1)}, u32[]{:S(2)}, u32[]{:S(2)}) async-start(bf16[128,8,2560]{2,1,0:T(8,128)(2,1)} %stack.20), calls=%async_computation.1 | async-start | bytes 10485760 | tf_op jit(solution)/shard_map/all_to_all | solution.py:17
  326.9 2.5 copy-start
  331.2 14.9 %collective-permute-start.1 = (bf16[2,512,128]{2,1,0:T(8,128)(2,1)S(1)}, bf16[2,512,128]{2,1,0:T(8,128)(2,1)S(1)}, u32[]{:S(2)}, u32[]{:S(2)}) collective-permute-start(bf16[2,512,128]{2,1,0:T(8,128)(2,1)S(1)} %get-tuple-element.120), channel_id=1, source_target_pairs={{4,0},{8,4},{12,8},{16,12},{20,16},{24,20},{28,24},{32,28},{36,32}... | collective-permute-start | bytes 786440 | tf_op jit(solution)/shard_map/ppermute | solution.py:51
  339.4 15.9 %collective-permute-start = (bf16[2,512,128]{2,1,0:T(8,128)(2,1)S(1)}, bf16[2,512,128]{2,1,0:T(8,128)(2,1)S(1)}, u32[]{:S(2)}, u32[]{:S(2)}) collective-permute-start(bf16[2,512,128]{2,1,0:T(8,128)(2,1)S(1)} %get-tuple-element.119), channel_id=1, source_target_pairs={{0,4},{4,8},{8,12},{12,16},{16,20},{20,24},{24,28},{28,32},{32,36}... | collective-permute-start | bytes 786440 | tf_op jit(solution)/shard_map/ppermute | solution.py:50
  359.5 20.1 %copy-start.5 = (bf16[256,256]{1,0:T(8,128)(2,1)S(1)}, bf16[256,256]{1,0:T(8,128)(2,1)}, u32[]{:S(2)}) copy-start(bf16[256,256]{1,0:T(8,128)(2,1)} %param.24) | copy-start | bytes 393220
  360.9 23.4 %copy-start.23 = (s32[2,4]{1,0:T(2,128)S(1)}, s32[2,4]{1,0:T(2,128)}, u32[]{:S(2)}) copy-start(s32[2,4]{1,0:T(2,128)} %param.41) | copy-start | bytes 100
  380.6 13.7 %all-to-all-start.4 = ((bf16[4,256,256]{1,2,0:T(8,128)(2,1)}), bf16[4,256,256]{1,2,0:T(8,128)(2,1)S(1)}, u32[]{:S(2)}, u32[]{:S(2)}) async-start(bf16[4,256,256]{1,2,0:T(8,128)(2,1)} %broadcast_in_dim.177), calls=%async_computation.4 | async-start | bytes 1048576 | tf_op jit(solution)/shard_map/all_to_all | solution.py:36
  397.5 7.7 %collective-permute-start.3 = (bf16[2,256,128]{2,1,0:T(8,128)(2,1)S(1)}, bf16[2,256,128]{2,1,0:T(8,128)(2,1)S(1)}, u32[]{:S(2)}, u32[]{:S(2)}) collective-permute-start(bf16[2,256,128]{2,1,0:T(8,128)(2,1)S(1)} %pad_maximum_fusion.4), channel_id=1, source_target_pairs={{4,0},{8,4},{12,8},{16,12},{20,16},{24,20},{28,24},{32,28},{36,32}... | collective-permute-start | bytes 393224 | tf_op jit(solution)/shard_map/ppermute | solution.py:51
  399.4 15.8 %collective-permute-start.2 = (bf16[2,256,128]{2,1,0:T(8,128)(2,1)S(1)}, bf16[2,256,128]{2,1,0:T(8,128)(2,1)S(1)}, u32[]{:S(2)}, u32[]{:S(2)}) collective-permute-start(bf16[2,256,128]{2,1,0:T(8,128)(2,1)S(1)} %pad_maximum_fusion.4), channel_id=1, source_target_pairs={{0,4},{4,8},{8,12},{12,16},{16,20},{20,24},{24,28},{28,32},{32,36}... | collective-permute-start | bytes 393224 | tf_op jit(solution)/shard_map/ppermute | solution.py:50
  459.5 20.8 %copy-start.21 = (s32[8,3]{0,1:T(4,128)S(1)}, s32[8,3]{0,1:T(4,128)}, u32[]{:S(2)}) copy-start(s32[8,3]{0,1:T(4,128)} %param.42) | copy-start | bytes 292
  459.6 21.0 %copy-start.25 = (s32[8]{0:T(128)S(1)}, s32[8]{0:T(128)}, u32[]{:S(2)}) copy-start(s32[8]{0:T(128)} %param.43) | copy-start | bytes 100
  475.9 0.9 copy-start.6
  476.8 13.7 %all-to-all-start.8 = ((bf16[4,256,256]{1,2,0:T(8,128)(2,1)}), bf16[4,256,256]{1,2,0:T(8,128)(2,1)S(1)}, u32[]{:S(2)}, u32[]{:S(2)}) async-start(bf16[4,256,256]{1,2,0:T(8,128)(2,1)} %broadcast_in_dim.185), calls=%async_computation.8 | async-start | bytes 1048576 | tf_op jit(solution)/shard_map/all_to_all | solution.py:36
  480.3 17.9 %copy-start.1 = (bf16[1024,1024]{0,1:T(8,128)(2,1)S(1)}, bf16[1024,1024]{0,1:T(8,128)(2,1)}, u32[]{:S(2)}) copy-start(bf16[1024,1024]{0,1:T(8,128)(2,1)} %fusion.8) | copy-start | bytes 6291460
  493.6 6.3 %collective-permute-start.5 = (bf16[2,128,128]{2,1,0:T(8,128)(2,1)S(1)}, bf16[2,128,128]{2,1,0:T(8,128)(2,1)S(1)}, u32[]{:S(2)}, u32[]{:S(2)}) collective-permute-start(bf16[2,128,128]{2,1,0:T(8,128)(2,1)S(1)} %get-tuple-element.122), channel_id=1, source_target_pairs={{4,0},{8,4},{12,8},{16,12},{20,16},{24,20},{28,24},{32,28},{36,32}... | collective-permute-start | bytes 196616 | tf_op jit(solution)/shard_map/ppermute | solution.py:51
  495.6 13.7 %collective-permute-start.4 = (bf16[2,128,128]{2,1,0:T(8,128)(2,1)S(1)}, bf16[2,128,128]{2,1,0:T(8,128)(2,1)S(1)}, u32[]{:S(2)}, u32[]{:S(2)}) collective-permute-start(bf16[2,128,128]{2,1,0:T(8,128)(2,1)S(1)} %get-tuple-element.121), channel_id=1, source_target_pairs={{0,4},{4,8},{8,12},{12,16},{16,20},{20,24},{24,28},{28,32},{32,36}... | collective-permute-start | bytes 196616 | tf_op jit(solution)/shard_map/ppermute | solution.py:50
  510.6 0.7 copy-start.2
  513.4 2.8 copy-start.3
  516.2 0.7 copy-start.2
  519.0 2.8 copy-start.3
